TPU v7x, 32 devices: a whole 2x2x4 slice. The times are simulated.
32 devices in a mesh: dp: 16 (over z, x, core), rows: 2 (over y).
Axes of the slice: x: 2, y: 2, z: 4, core: 2. Of those that a mesh axis runs over, the one named last changes fastest.
Arguments:
- fine_level: bfloat16 [16, 32, 64, 256], P('dp', 'rows'), may hold values from -6 to 6
- out_grad: bfloat16 [16, 32, 64, 256], P('dp', 'rows'), may hold values from -6 to 6
- fine_input: bfloat16 [16, 32, 64, 256], P('dp', 'rows'), may hold values from -6 to 6
- mid_input: bfloat16 [16, 16, 32, 512], P('dp', None, None, 'rows'), may hold values from -6 to 6
- top_input: bfloat16 [16, 8, 16, 1024], P('dp', None, None, 'rows'), may hold values from -6 to 6
- smooth_weight: bfloat16 [3, 3, 256, 256], replicated, may hold values from -0.125 to 0.125
- fine_lateral: bfloat16 [256, 256], replicated, may hold values from -0.375 to 0.375
- mid_lateral: bfloat16 [512, 256], P('rows'), may hold values from -0.375 to 0.375
- top_lateral: bfloat16 [1024, 256], P('rows'), may hold values from -0.375 to 0.375
Outputs:
- grad_fine: bfloat16 [16, 32, 64, 256], P('dp', 'rows')
- grad_mid: bfloat16 [16, 16, 32, 512], P('dp', None, None, 'rows')
- grad_top: bfloat16 [16, 8, 16, 1024], P('dp', None, None, 'rows')
- kernel_grads: float32 [2560, 256], P('dp')
- midlat_grad: float32 [512, 256], P('rows')
- toplat_grad: float32 [1024, 256], P('rows')
All inputs are finite; a program needn't handle non-finite values.
Results may differ from a plain program's by a relative error of at most 0.0062.
Values may be sent and summed in bfloat16 or wider, within the bound.
No kernel may reach another device: no remote copies, remote signals or barrier semaphores. Data moves between devices by JAX's collectives and lax.ppermute only.
A program may use at most 64 MiB of HBM per device.

v0:
```python
import jax
import jax.numpy as jnp
from jax import lax
from jax.sharding import PartitionSpec as P


def with_halo(value, sides, width):
    for axis, dim in sides:
        count, length = (lax.axis_size(axis), value.shape[dim])
        up = [(i, (i + 1) % count) for i in range(count - 1)]
        down = [(j, i) for i, j in up]
        last = lax.slice_in_dim(value, length - width, length, axis=dim)
        leading = lax.slice_in_dim(value, 0, width, axis=dim)
        before = lax.ppermute(last, axis, up)
        after = lax.ppermute(leading, axis, down)
        value = jnp.concatenate([before, value, after], axis=dim)
    return value


def pool_two(field):
    images, rows_n, cols_n, chans = field.shape
    return field.reshape(images, rows_n // 2, 2, cols_n // 2, 2, chans).sum(axis=(2, 4))


def contract_last(left, right):
    return lax.dot_general(
        left, right, (((1,), (1,)), ((), ())), preferred_element_type=jnp.float32
    )


def contract_first(left, right):
    return lax.dot_general(
        left, right, (((0,), (0,)), ((), ())), preferred_element_type=jnp.float32
    )


def body(
    fine_level,
    out_grad,
    fine_input,
    mid_input,
    top_input,
    smooth_weight,
    fine_lateral,
    mid_lateral,
    top_lateral,
):
    images, strip, width, chans = out_grad.shape
    cells = images * strip * width
    rimmed = with_halo(out_grad, (("rows", 1),), 1)
    rimmed = jnp.pad(rimmed, ((0, 0), (0, 0), (1, 1), (0, 0)))
    fine_flat = fine_level.reshape(cells, chans)
    level_grad = jnp.zeros((cells, chans), jnp.float32)
    pieces = []
    for tap_a in range(3):
        for tap_b in range(3):
            shifted = rimmed[
                :, 2 - tap_a : 2 - tap_a + strip, 2 - tap_b : 2 - tap_b + width, :
            ].reshape(cells, chans)
            level_grad = level_grad + contract_last(shifted, smooth_weight[tap_a, tap_b])
            pieces.append(contract_first(fine_flat, shifted))
    fine_grad = level_grad.astype(jnp.bfloat16)
    grad_fine = (
        contract_last(fine_grad, fine_lateral)
        .astype(jnp.bfloat16)
        .reshape(images, strip, width, -1)
    )
    pieces.append(contract_first(fine_input.reshape(cells, -1), fine_grad))
    kernel_term = jnp.concatenate(pieces, axis=0)
    share = lax.psum_scatter(kernel_term, "dp", scatter_dimension=0, tiled=True)
    kernel_grads = lax.psum(share, "rows")
    pooled = pool_two(level_grad.reshape(images, strip, width, chans)).astype(jnp.bfloat16)
    mid_grad = lax.all_gather(pooled, "rows", axis=1, tiled=True)
    top_grad = pool_two(mid_grad.astype(jnp.float32)).astype(jnp.bfloat16)
    mid_flat = mid_grad.reshape(-1, chans)
    top_flat = top_grad.reshape(-1, chans)
    grad_mid = contract_last(mid_flat, mid_lateral).astype(jnp.bfloat16).reshape(mid_input.shape)
    grad_top = contract_last(top_flat, top_lateral).astype(jnp.bfloat16).reshape(top_input.shape)
    mid_term = contract_first(mid_input.reshape(mid_flat.shape[0], -1), mid_flat)
    top_term = contract_first(top_input.reshape(top_flat.shape[0], -1), top_flat)
    midlat_grad, toplat_grad = lax.psum((mid_term, top_term), "dp")
    return (grad_fine, grad_mid, grad_top, kernel_grads, midlat_grad, toplat_grad)


def solution(mesh):
    placed = (
        P("dp", "rows", None, None),
        P("dp", "rows", None, None),
        P("dp", "rows", None, None),
        P("dp", None, None, "rows"),
        P("dp", None, None, "rows"),
        P(),
        P(),
        P("rows", None),
        P("rows", None),
    )
    return jax.shard_map(
        body,
        mesh=mesh,
        in_specs=placed,
        out_specs=(
            P("dp", "rows", None, None),
            P("dp", None, None, "rows"),
            P("dp", None, None, "rows"),
            P("dp", None),
            P("rows", None),
            P("rows", None),
        ),
        check_vma=False,
    )
```

profile of v0, /device:TPU:0, one launch (start us, length us, event | category | flops | bytes accessed | tf_op | source)
XLA Modules:
  0.0 226.8 jit_solution(9523882617823128854)
XLA Ops:
  7.2 0.0 copy-start
  7.2 0.0 reduce-scatter.2.cloned.1.call-start
  7.2 0.8 fusion.66
  8.1 4.9 %collective-permute-start = (bf16[1,1,64,256]{3,2,1,0:T(8,128)(2,1)S(1)}, bf16[1,1,64,256]{3,2,1,0:T(8,128)(2,1)S(1)}, u32[]{:S(2)}, u32[]{:S(2)}) collective-permute-start(bf16[1,1,64,256]{3,2,1,0:T(8,128)(2,1)S(1)} %get-tuple-element.28), channel_id=1, source_target_pairs={{0,1},{2,3},{4,5},{6,7},{8,9},{10,11},{12,13},{14,15},{16,17},{18,... | collective-permute-start | bytes 98312 | tf_op jit(solution)/shard_map/ppermute | solution.py:14
  13.0 1.3 collective-permute-start.1
  14.3 0.3 collective-permute-done
  14.5 4.2 %collective-permute-done.1 = bf16[1,1,64,256]{3,2,1,0:T(8,128)(2,1)S(1)} collective-permute-done((bf16[1,1,64,256]{3,2,1,0:T(8,128)(2,1)S(1)}, bf16[1,1,64,256]{3,2,1,0:T(8,128)(2,1)S(1)}, u32[]{:S(2)}, u32[]{:S(2)}) %collective-permute-start.1) | collective-permute-done | bytes 32800 | tf_op jit(solution)/shard_map/ppermute | solution.py:15
  18.8 1.3 fusion.16
  20.0 0.0 copy-start.1
  20.1 0.5 fusion.65
  20.6 0.0 copy-done
  20.6 1.1 fusion.11
  21.7 0.0 copy-done.1
  21.7 0.1 pad_maximum_fusion
  21.8 1.1 fusion.10
  22.8 1.0 fusion.9
  23.9 1.1 fusion.8
  24.9 1.0 fusion.7
  26.0 1.1 fusion.6
  27.0 1.1 fusion.5
  28.1 1.1 fusion.4
  29.2 1.0 fusion.3
  30.3 0.0 copy-done.2
  30.3 0.3 fusion.48
  30.6 0.3 fusion.39
  30.9 0.3 convolution_add_fusion.6
  31.3 0.3 convolution_add_fusion.5
  31.6 0.3 convolution_add_fusion.4
  31.9 0.3 convolution_add_fusion.3
  32.3 0.3 convolution_add_fusion.2
  32.6 0.0 copy-start.3
  32.6 0.3 convolution_add_fusion.1
  33.0 0.3 fusion
  33.3 0.4 copy-done.3
  33.7 1.1 fusion.2
  34.7 0.0 reduce-scatter.2.cloned.1.call-update
  34.7 0.0 copy-start.8
  34.7 0.0 copy-start.7
  34.8 0.0 all-reduce.7.cloned.1.call-start
  34.8 0.6 reshape_reshape.3
  35.4 0.9 reduce_sum.18
  36.3 5.6 %all-gather = bf16[16,32,256]{2,1,0:T(8,128)(2,1)S(1)} all-gather(bf16[8,32,256]{2,1,0:T(8,128)(2,1)S(1)} %reduce_sum.18), channel_id=2, replica_groups=mesh['dp'=16,'rows'=2] {'rows'}, dimensions={0}, use_global_device_ids=true | all-gather | bytes 393216 | tf_op jit(solution)/shard_map/all_gather | solution.py:73
  41.9 0.1 reshape.142
  42.0 0.0 copy-start.6
  42.0 0.5 reduce.2
  42.5 0.0 copy-done.8
  42.5 1.0 convolution_bitcast_fusion
  43.6 0.0 copy-done.7
  43.6 1.0 convolution_bitcast_fusion.1
  44.5 0.0 all-reduce.7.cloned.1.call-update
  44.6 0.0 all-reduce.5.cloned.1.call-start
  44.6 0.0 copy-done.5
  44.6 1.0 convolution_convert_fusion.1
  45.6 0.0 copy-done.6
  45.6 1.1 convolution_convert_fusion
  46.7 52.6 %reduce-scatter.2.cloned.1.call-done = f32[160,256]{1,0:T(8,128)} async-done(((f32[2560,256]{1,0:T(8,128)}), f32[160,256]{1,0:T(8,128)}) %reduce-scatter.2.cloned.1.call-update) | async-done | bytes 163856 | tf_op jit(solution)/shard_map/reduce_scatter | solution.py:70
  99.3 0.0 all-reduce.5.cloned.1.call-update
  99.4 0.0 copy-done.4
  99.4 0.9 convolution_convert_fusion.2
  100.3 95.1 %all-reduce.7.cloned.1.call-done = (f32[256,256]{0,1:T(8,128)}, f32[512,256]{0,1:T(8,128)}) async-done(((f32[256,256]{0,1:T(8,128)}, f32[512,256]{0,1:T(8,128)}), (f32[256,256]{0,1:T(8,128)}, f32[512,256]{0,1:T(8,128)})) %all-reduce.7.cloned.1.call-update) | async-done | bytes 786448 | tf_op jit(solution)/shard_map/psum | solution.py:81
  195.4 1.8 copy.17
  197.1 2.0 copy.18
  199.2 19.5 %all-reduce.5.cloned.1.call-done = f32[160,256]{1,0:T(8,128)} async-done(((f32[160,256]{1,0:T(8,128)}), f32[160,256]{1,0:T(8,128)}) %all-reduce.5.cloned.1.call-update) | async-done | bytes 163856 | tf_op jit(solution)/shard_map/psum | solution.py:71
  218.7 1.6 copy.31
  (3 shorter events, 0.0 us)
Async XLA Ops:
  7.2 13.4 %copy-start = (bf16[1,16,64,256]{3,2,1,0:T(8,128)(2,1)S(1)}, bf16[1,16,64,256]{3,2,1,0:T(8,128)(2,1)}, u32[]{:S(2)}) copy-start(bf16[1,16,64,256]{3,2,1,0:T(8,128)(2,1)} %param.9) | copy-start | bytes 1572868
  7.2 92.2 %reduce-scatter.2.cloned.1.call-start = ((), (), s32[]{:S(2)}) async-start(), calls=%async_computation.1 | async-start | bytes 2785280 | tf_op jit(solution)/shard_map/reduce_scatter | solution.py:70
  8.1 6.5 %collective-permute-start = (bf16[1,1,64,256]{3,2,1,0:T(8,128)(2,1)S(1)}, bf16[1,1,64,256]{3,2,1,0:T(8,128)(2,1)S(1)}, u32[]{:S(2)}, u32[]{:S(2)}) collective-permute-start(bf16[1,1,64,256]{3,2,1,0:T(8,128)(2,1)S(1)} %get-tuple-element.28), channel_id=1, source_target_pairs={{0,1},{2,3},{4,5},{6,7},{8,9},{10,11},{12,13},{14,15},{16,17},{18,... | collective-permute-start | bytes 98312 | tf_op jit(solution)/shard_map/ppermute | solution.py:14
  13.0 5.8 %collective-permute-start.1 = (bf16[1,1,64,256]{3,2,1,0:T(8,128)(2,1)S(1)}, bf16[1,1,64,256]{3,2,1,0:T(8,128)(2,1)S(1)}, u32[]{:S(2)}, u32[]{:S(2)}) collective-permute-start(bf16[1,1,64,256]{3,2,1,0:T(8,128)(2,1)S(1)} %get-tuple-element.29), channel_id=1, source_target_pairs={{1,0},{3,2},{5,4},{7,6},{9,8},{11,10},{13,12},{15,14},{17,16},{19,... | collective-permute-start | bytes 98312 | tf_op jit(solution)/shard_map/ppermute | solution.py:15
  20.0 1.7 copy-start.1
  27.0 3.2 %copy-start.2 = (bf16[3,3,256,256]{3,2,1,0:T(8,128)(2,1)S(1)}, bf16[3,3,256,256]{3,2,1,0:T(8,128)(2,1)}, u32[]{:S(2)}) copy-start(bf16[3,3,256,256]{3,2,1,0:T(8,128)(2,1)} %param.14) | copy-start | bytes 3538948
  32.6 1.0 copy-start.3
  34.7 7.8 %copy-start.8 = (bf16[1,8,16,512]{3,2,1,0:T(8,128)(2,1)S(1)}, bf16[1,8,16,512]{3,2,1,0:T(8,128)(2,1)}, u32[]{:S(2)}) copy-start(bf16[1,8,16,512]{3,2,1,0:T(8,128)(2,1)} %param.13) | copy-start | bytes 393220
  34.7 8.8 %copy-start.7 = (bf16[1,16,32,256]{3,2,1,0:T(8,128)(2,1)S(1)}, bf16[1,16,32,256]{3,2,1,0:T(8,128)(2,1)}, u32[]{:S(2)}) copy-start(bf16[1,16,32,256]{3,2,1,0:T(8,128)(2,1)} %param.12) | copy-start | bytes 786436
  34.8 160.6 %all-reduce.7.cloned.1.call-start = ((), (), s32[]{:S(2)}) async-start(), calls=%async_computation.3 | async-start | bytes 1572864 | tf_op jit(solution)/shard_map/psum | solution.py:81
  41.9 2.7 %copy-start.5 = (bf16[256,256]{1,0:T(8,128)(2,1)S(1)}, bf16[256,256]{1,0:T(8,128)(2,1)}, u32[]{:S(2)}) copy-start(bf16[256,256]{1,0:T(8,128)(2,1)} %param.16) | copy-start | bytes 393220
  42.0 3.5 %copy-start.6 = (bf16[256,256]{1,0:T(8,128)(2,1)S(1)}, bf16[256,256]{1,0:T(8,128)(2,1)}, u32[]{:S(2)}) copy-start(bf16[256,256]{1,0:T(8,128)(2,1)} %param.15) | copy-start | bytes 393220
  43.6 55.8 %copy-start.4 = (bf16[512,256]{1,0:T(8,128)(2,1)S(1)}, bf16[512,256]{1,0:T(8,128)(2,1)}, u32[]{:S(2)}) copy-start(bf16[512,256]{1,0:T(8,128)(2,1)} %param.17) | copy-start | bytes 786436
  44.6 174.2 %all-reduce.5.cloned.1.call-start = ((), (), s32[]{:S(2)}) async-start(), calls=%async_computation.2 | async-start | bytes 327680 | tf_op jit(solution)/shard_map/psum | solution.py:71
Sparse Core Ops, SparseCore 0:
  34.8 64.4 reduce-scatter.1
  103.4 91.8 all-reduce.6
  197.6 21.0 all-reduce.4
where the time goes:
time: 227 us
  waiting for transfers between devices  172 us (76%)
  matrix products  18.6 us (8%)
  between operations  13.9 us (6%)
  local copies, waits for them, and re-layouts  7.89 us (3%)
  starting transfers between devices  6.3 us (3%)
  blocking collectives  5.64 us (2%)
  other arithmetic  2.65 us (1%)
    psum x1, waiting for transfers between devices, body(): midlat_grad, toplat_grad = lax.psum((mid_term, top_term), 'dp')  95.1 us
    reduce_scatter x1, waiting for transfers between devices, body(): share = lax.psum_scatter(kernel_term, 'dp', scatter_dimension=0, tiled=True)  52.6 us
    psum x1, waiting for transfers between devices, body(): kernel_grads = lax.psum(share, 'rows')  19.5 us
    dot_general x12, matrix products, contract_first(): lax.dot_general(left, right, (((0,), (0,)), ((), ())), preferred_element_...  12.6 us
    dot_general x12, matrix products, contract_last(): lax.dot_general(left, right, (((1,), (1,)), ((), ())), preferred_element_...  5.95 us
    unnamed x21, local copies, waits for them, and re-layouts  5.82 us
    all_gather x1, blocking collectives, body(): mid_grad = lax.all_gather(pooled, 'rows', axis=1, tiled=True)  5.64 us
    ppermute x1, starting transfers between devices, with_halo(): before = lax.ppermute(last, axis, up)  4.89 us
  transfers between devices with their start and end apart: 5, of which 5 were waited for; matrix products, arithmetic and copies ran while one was open for 5% of the time, Pallas kernels for 0%

commit v1 on v0

--- a/solution.py
+++ b/solution.py
@@ -2,6 +2,7 @@
 import jax.numpy as jnp
 from jax import lax
 from jax.sharding import PartitionSpec as P
+from jax.lax import all_gather
 
 
 def with_halo(value, sides, width):
@@ -68,7 +69,11 @@
     pieces.append(contract_first(fine_input.reshape(cells, -1), fine_grad))
     kernel_term = jnp.concatenate(pieces, axis=0)
     share = lax.psum_scatter(kernel_term, "dp", scatter_dimension=0, tiled=True)
-    kernel_grads = lax.psum(share, "rows")
+
+    def bind_space(local_values):
+        return jnp.sum(all_gather(local_values, "rows"), axis=0)
+
+    kernel_grads = bind_space(share)
     pooled = pool_two(level_grad.reshape(images, strip, width, chans)).astype(jnp.bfloat16)
     mid_grad = lax.all_gather(pooled, "rows", axis=1, tiled=True)
     top_grad = pool_two(mid_grad.astype(jnp.float32)).astype(jnp.bfloat16)

time: 227 us -> 214 us (0.943)
  waiting for transfers between devices: 172 us -> 156 us
  blocking collectives: 5.64 us -> 11.8 us
  matrix products: 18.6 us -> 14 us
    psum x1 -> x0, waiting for transfers between devices: 19.5 us -> none  [body(): kernel_grads = lax.psum(share, 'rows')]
    reduce_scatter x1, waiting for transfers between devices: 52.6 us -> 63.2 us  [body(): share = lax.psum_scatter(kernel_term, 'dp', scatter_dimension=0, tiled=True)]
    psum x1, waiting for transfers between devices: 95.1 us -> 88.2 us  [body(): midlat_grad, toplat_grad = lax.psum((mid_term, top_term), 'dp')]
    all_gather x0 -> x1, blocking collectives: none -> 6.19 us  [bind_space(): return jnp.sum(all_gather(local_values, 'rows'), axis=0)]
    dot_general x12, matrix products: 12.6 us -> 8.03 us  [contract_first(): lax.dot_general(left, right, (((0,), (0,)), ((), ())), preferred_element_...]
    unnamed x21 -> x20, local copies, waits for them, and re-layouts: 5.82 us -> 5.65 us
  transfers between devices with their start and end apart: 5 -> 4, of which waited for: 5 -> 4; matrix products, arithmetic and copies ran while one was open for 5% -> 4% of each run, Pallas kernels for 0% -> 0%
where the time goes in v1:
time: 214 us; the launch traced here: 213 us
  waiting for transfers between devices  156 us (73%)
  between operations  14.3 us (7%)
  matrix products  14 us (7%)
  blocking collectives  11.8 us (6%)
  local copies, waits for them, and re-layouts  7.72 us (4%)
  starting transfers between devices  6.26 us (3%)
  other arithmetic  3.4 us (2%)
    psum x1, waiting for transfers between devices, body(): midlat_grad, toplat_grad = lax.psum((mid_term, top_term), 'dp')  88.2 us
    reduce_scatter x1, waiting for transfers between devices, body(): share = lax.psum_scatter(kernel_term, 'dp', scatter_dimension=0, tiled=True)  63.2 us
    dot_general x12, matrix products, contract_first(): lax.dot_general(left, right, (((0,), (0,)), ((), ())), preferred_element_...  8.03 us
    all_gather x1, blocking collectives, bind_space(): return jnp.sum(all_gather(local_values, 'rows'), axis=0)  6.19 us
    dot_general x12, matrix products, contract_last(): lax.dot_general(left, right, (((1,), (1,)), ((), ())), preferred_element_...  5.93 us
    unnamed x20, local copies, waits for them, and re-layouts  5.65 us
    all_gather x1, blocking collectives, body(): mid_grad = lax.all_gather(pooled, 'rows', axis=1, tiled=True)  5.64 us
    ppermute x1, starting transfers between devices, with_halo(): before = lax.ppermute(last, axis, up)  4.89 us
  transfers between devices with their start and end apart: 4, of which 4 were waited for; matrix products, arithmetic and copies ran while one was open for 4% of the time, Pallas kernels for 0%

profile of v1, /device:TPU:0, one launch (start us, length us, event | category | flops | bytes accessed | tf_op | source)
XLA Modules:
  0.0 213.4 jit_solution(14202523876867171814)
XLA Ops:
  7.2 0.0 copy-start
  7.2 0.0 all-reduce.4.cloned.1.call-start
  7.2 0.8 fusion.66
  8.1 4.9 %collective-permute-start = (bf16[1,1,64,256]{3,2,1,0:T(8,128)(2,1)S(1)}, bf16[1,1,64,256]{3,2,1,0:T(8,128)(2,1)S(1)}, u32[]{:S(2)}, u32[]{:S(2)}) collective-permute-start(bf16[1,1,64,256]{3,2,1,0:T(8,128)(2,1)S(1)} %get-tuple-element.28), channel_id=1, source_target_pairs={{0,1},{2,3},{4,5},{6,7},{8,9},{10,11},{12,13},{14,15},{16,17},{18,... | collective-permute-start | bytes 98312 | tf_op jit(solution)/shard_map/ppermute | solution.py:15
  13.0 1.3 collective-permute-start.1
  14.3 0.3 collective-permute-done
  14.5 4.2 %collective-permute-done.1 = bf16[1,1,64,256]{3,2,1,0:T(8,128)(2,1)S(1)} collective-permute-done((bf16[1,1,64,256]{3,2,1,0:T(8,128)(2,1)S(1)}, bf16[1,1,64,256]{3,2,1,0:T(8,128)(2,1)S(1)}, u32[]{:S(2)}, u32[]{:S(2)}) %collective-permute-start.1) | collective-permute-done | bytes 32800 | tf_op jit(solution)/shard_map/ppermute | solution.py:16
  18.8 1.3 fusion.16
  20.0 0.0 copy-start.1
  20.1 0.5 fusion.65
  20.6 0.0 copy-done
  20.6 0.4 fusion.11
  21.0 0.1 copy-done.1
  21.1 0.1 pad_maximum_fusion
  21.2 0.4 fusion.10
  21.5 0.3 fusion.9
  21.9 0.4 fusion.8
  22.3 0.0 copy-start.3
  22.3 0.3 fusion.7
  22.6 0.3 fusion.6
  23.0 0.4 fusion.5
  23.4 0.2 copy-done.3
  23.5 0.3 fusion.48
  23.9 0.3 fusion.39
  24.2 0.4 fusion.4
  24.6 0.0 copy-start.2
  24.6 1.5 copy-done.2
  26.1 0.3 convolution_add_fusion.6
  26.4 0.3 convolution_add_fusion.5
  26.8 0.3 convolution_add_fusion.4
  27.1 0.3 convolution_add_fusion.3
  27.4 0.3 convolution_add_fusion.2
  27.8 0.3 convolution_add_fusion.1
  28.1 0.3 fusion
  28.4 0.6 reshape_reshape.3
  29.1 0.0 copy-start.8
  29.1 0.9 reduce_sum.27
  30.0 5.6 %all-gather = bf16[16,32,256]{2,1,0:T(8,128)(2,1)S(1)} all-gather(bf16[8,32,256]{2,1,0:T(8,128)(2,1)S(1)} %reduce_sum.27), channel_id=2, replica_groups=mesh['dp'=16,'rows'=2] {'rows'}, dimensions={0}, use_global_device_ids=true | all-gather | bytes 393216 | tf_op jit(solution)/shard_map/all_gather | solution.py:78
  35.6 0.1 reshape.142
  35.7 0.0 copy-start.4
  35.7 2.0 convolution_bitcast_fusion.1
  37.7 0.5 reduce.2
  38.2 0.0 copy-done.8
  38.2 1.0 convolution_bitcast_fusion
  39.2 0.0 all-reduce.4.cloned.1.call-update
  39.3 0.0 copy-start.5
  39.3 0.0 reduce-scatter.2.cloned.1.call-start
  39.3 1.0 fusion.3
  40.4 0.0 copy-start.6
  40.4 0.0 copy-done.4
  40.4 1.1 fusion.2
  41.4 0.0 reduce-scatter.2.cloned.1.call-update
  41.5 0.0 copy-done.5
  41.5 0.9 convolution_convert_fusion.2
  42.4 0.0 copy-done.6
  42.4 1.0 convolution_convert_fusion.1
  43.3 0.0 copy-done.7
  43.3 1.1 convolution_convert_fusion
  44.5 88.2 %all-reduce.4.cloned.1.call-done = (f32[256,256]{0,1:T(8,128)}, f32[512,256]{0,1:T(8,128)}) async-done(((f32[256,256]{0,1:T(8,128)}, f32[512,256]{0,1:T(8,128)}), (f32[256,256]{0,1:T(8,128)}, f32[512,256]{0,1:T(8,128)})) %all-reduce.4.cloned.1.call-update) | async-done | bytes 786448 | tf_op jit(solution)/shard_map/psum | solution.py:86
  132.6 1.8 copy.17
  134.4 2.0 copy.18
  136.4 63.2 %reduce-scatter.2.cloned.1.call-done = f32[160,256]{1,0:T(8,128)} async-done(((f32[2560,256]{1,0:T(8,128)}), f32[160,256]{1,0:T(8,128)}) %reduce-scatter.2.cloned.1.call-update) | async-done | bytes 163856 | tf_op jit(solution)/shard_map/reduce_scatter | solution.py:71
  199.7 6.2 %all-gather.1 = f32[320,256]{1,0:T(8,128)S(1)} all-gather(f32[160,256]{1,0:T(8,128)} %reduce-scatter.2.cloned.1.call-done), channel_id=3, replica_groups=mesh['dp'=16,'rows'=2] {'rows'}, dimensions={0}, use_global_device_ids=true | all-gather | bytes 491520 | tf_op jit(solution)/shard_map/all_gather | solution.py:74
  205.9 0.7 reduce_sum.29
  (1 shorter events, 0.0 us)
Async XLA Ops:
  7.2 13.4 %copy-start = (bf16[1,16,64,256]{3,2,1,0:T(8,128)(2,1)S(1)}, bf16[1,16,64,256]{3,2,1,0:T(8,128)(2,1)}, u32[]{:S(2)}) copy-start(bf16[1,16,64,256]{3,2,1,0:T(8,128)(2,1)} %param.9) | copy-start | bytes 1572868
  7.2 125.4 %all-reduce.4.cloned.1.call-start = ((), (), s32[]{:S(2)}) async-start(), calls=%async_computation.2 | async-start | bytes 1572864 | tf_op jit(solution)/shard_map/psum | solution.py:86
  8.1 6.5 %collective-permute-start = (bf16[1,1,64,256]{3,2,1,0:T(8,128)(2,1)S(1)}, bf16[1,1,64,256]{3,2,1,0:T(8,128)(2,1)S(1)}, u32[]{:S(2)}, u32[]{:S(2)}) collective-permute-start(bf16[1,1,64,256]{3,2,1,0:T(8,128)(2,1)S(1)} %get-tuple-element.28), channel_id=1, source_target_pairs={{0,1},{2,3},{4,5},{6,7},{8,9},{10,11},{12,13},{14,15},{16,17},{18,... | collective-permute-start | bytes 98312 | tf_op jit(solution)/shard_map/ppermute | solution.py:15
  13.0 5.8 %collective-permute-start.1 = (bf16[1,1,64,256]{3,2,1,0:T(8,128)(2,1)S(1)}, bf16[1,1,64,256]{3,2,1,0:T(8,128)(2,1)S(1)}, u32[]{:S(2)}, u32[]{:S(2)}) collective-permute-start(bf16[1,1,64,256]{3,2,1,0:T(8,128)(2,1)S(1)} %get-tuple-element.29), channel_id=1, source_target_pairs={{1,0},{3,2},{5,4},{7,6},{9,8},{11,10},{13,12},{15,14},{17,16},{19,... | collective-permute-start | bytes 98312 | tf_op jit(solution)/shard_map/ppermute | solution.py:16
  20.0 1.0 copy-start.1
  22.3 1.3 copy-start.3
  24.6 1.5 copy-start.2
  29.1 9.1 %copy-start.8 = (bf16[1,8,16,512]{3,2,1,0:T(8,128)(2,1)S(1)}, bf16[1,8,16,512]{3,2,1,0:T(8,128)(2,1)}, u32[]{:S(2)}) copy-start(bf16[1,8,16,512]{3,2,1,0:T(8,128)(2,1)} %param.13) | copy-start | bytes 393220
  35.7 4.7 %copy-start.4 = (bf16[1,16,64,256]{3,2,1,0:T(8,128)(2,1)S(1)}, bf16[1,16,64,256]{3,2,1,0:T(8,128)(2,1)}, u32[]{:S(2)}) copy-start(bf16[1,16,64,256]{3,2,1,0:T(8,128)(2,1)} %param.11) | copy-start | bytes 1572868
  39.3 2.2 %copy-start.5 = (bf16[512,256]{1,0:T(8,128)(2,1)S(1)}, bf16[512,256]{1,0:T(8,128)(2,1)}, u32[]{:S(2)}) copy-start(bf16[512,256]{1,0:T(8,128)(2,1)} %param.17) | copy-start | bytes 786436
  39.3 160.4 %reduce-scatter.2.cloned.1.call-start = ((), (), s32[]{:S(2)}) async-start(), calls=%async_computation.1 | async-start | bytes 2785280 | tf_op jit(solution)/shard_map/reduce_scatter | solution.py:71
  40.4 2.0 copy-start.6
  40.4 2.9 %copy-start.7 = (bf16[256,256]{1,0:T(8,128)(2,1)S(1)}, bf16[256,256]{1,0:T(8,128)(2,1)}, u32[]{:S(2)}) copy-start(bf16[256,256]{1,0:T(8,128)(2,1)} %param.15) | copy-start | bytes 393220
Sparse Core Ops, SparseCore 0:
  39.4 93.1 all-reduce.3
  136.4 63.2 reduce-scatter.1
